TPU v7x, 16 devices: a whole 2x2x2 slice. The times are simulated.
16 devices in a mesh: dp: 4 (over z, y), dcp: 4 (over x, core).
Axes of the slice: x: 2, y: 2, z: 2, core: 2. Of those that a mesh axis runs over, the one named last changes fastest.
Arguments:
- q_abs: bfloat16 [128, 2, 64, 576], P('dp', None, 'dcp'), parts along dimension 0
- kv_cache: bfloat16 [128, 32, 4, 64, 576], P('dp', None, 'dcp'), parts along dimension 0
- lengths: int32 [128], P('dp'), parts along dimension 0
Outputs:
- output: bfloat16 [128, 2, 64, 512], P('dp', None, 'dcp'), parts along dimension 0
There are 4 independent parts. A program takes and returns all parts, laid end to end along the dimension named above; each array names one.
All inputs are finite; a program needn't handle non-finite values.
Results may differ from a plain program's by a relative error of at most 0.00786528.
Values are sent between devices in bfloat16 or wider.
A program may use at most 1 GiB of HBM per device.

v0:
```python
import jax
import jax.numpy as jnp
from jax import lax
from jax.sharding import PartitionSpec as P

LATENT = 512
ROPE = 64
NOPE = 128
PAGE = 64
MASKED = -1e30


def solution(mesh):
    group_size = mesh.shape['dcp']
    score_scale = (NOPE + ROPE) ** -0.5

    def local_step(q_blk, kv_blk, len_blk):
        batch_loc, tok_count, heads_loc, q_width = q_blk.shape
        rounds = kv_blk.shape[1]
        local_keys = kv_blk.reshape(batch_loc, rounds * PAGE, q_width)
        q_all = lax.all_gather(q_blk, 'dcp', axis=2, tiled=True)
        scores = jnp.einsum('bthd,bsd->bths', q_all, local_keys, preferred_element_type=jnp.float32) * score_scale
        device = lax.axis_index('dcp')
        positions = ((jnp.arange(rounds)[:, None] * group_size + device) * PAGE + jnp.arange(PAGE)[None, :]).reshape(rounds * PAGE)
        last_pos = len_blk[:, None] - tok_count + jnp.arange(tok_count)[None, :]
        visible = positions[None, None, None, :] <= last_pos[:, :, None, None]
        scores = jnp.where(visible, scores, MASKED)
        row_max = jnp.max(scores, axis=-1)
        weights = jnp.exp(scores - row_max[..., None])
        row_sum = jnp.sum(weights, axis=-1)
        part_out = jnp.einsum('bths,bsc->bthc', weights.astype(jnp.bfloat16), local_keys[:, :, :LATENT], preferred_element_type=jnp.float32)
        part_out = (part_out / row_sum[..., None]).astype(jnp.bfloat16)
        part_lse = row_max + jnp.log(row_sum)
        recv_out = lax.all_to_all(part_out, 'dcp', 2, 2, tiled=True).reshape(batch_loc, tok_count, group_size, heads_loc, LATENT)
        recv_lse = lax.all_to_all(part_lse, 'dcp', 2, 2, tiled=True).reshape(batch_loc, tok_count, group_size, heads_loc)
        total_lse = jax.nn.logsumexp(recv_lse, axis=2, keepdims=True)
        merge_w = jnp.exp(recv_lse - total_lse)
        merged = jnp.sum(merge_w[..., None] * recv_out.astype(jnp.float32), axis=2)
        return merged.astype(jnp.bfloat16)

    return jax.shard_map(local_step, mesh=mesh, in_specs=(P('dp', None, 'dcp', None), P('dp', None, 'dcp', None, None), P('dp')), out_specs=P('dp', None, 'dcp', None), check_vma=False)
```

profile of v0, /device:TPU:0, one launch (start us, length us, event | category | flops | bytes accessed | tf_op | source)
XLA Modules:
  0.0 229.2 jit_solution(12212572897418843012)
XLA Ops:
  6.5 0.0 all-gather.2.cloned.1.call-start
  6.5 0.7 all-gather.2.cloned.1.call-update
  7.3 0.1 iota_add_fusion.1
  7.3 0.1 add.66
  7.4 0.7 broadcast_add_fusion
  8.1 0.1 iota_add_fusion
  8.2 0.4 broadcast_compare_fusion
  8.5 41.7 %all-gather.2.cloned.1.call-done = bf16[32,2,64,576]{3,2,1,0:T(8,128)(2,1)} async-done(((bf16[32,2,16,576]{3,2,1,0:T(8,128)(2,1)}), bf16[32,2,64,576]{3,2,1,0:T(8,128)(2,1)}) %all-gather.2.cloned.1.call-update) | async-done | bytes 4718608 | tf_op jit(solution)/shard_map/all_gather | solution.py:21
  50.2 46.5 %fusion.1 = (f32[32,2,64]{2,1,0:T(2,128)S(1)}, f32[32,2,64,2048]{3,2,1,0:T(8,128)}) fusion(pred[32,2,2048]{2,1,0:T(4,128)(4,1)S(1)} %broadcast_compare_fusion, bf16[32,2,64,576]{3,2,1,0:T(8,128)(2,1)} %all-gather.2.cloned.1.call-done, bf16[32,2048,576,1]{2,1,3,0:T(8,128)(2,1)} %bitcast.7), kind=kOutput, calls=%fused_computation.4 | convolution fusion | flops 9688838144 | bytes 113917952 | tf_op jit(solution)/shard_map/bthd,bsd->bths/dot_general | solution.py:22
  96.7 15.0 %fusion.3 = f32[32,2,64]{2,1,0:T(2,128)S(1)} fusion(f32[32,2,64,2048]{3,2,1,0:T(8,128)} %get-tuple-element.6, f32[32,2,64]{2,1,0:T(2,128)S(1)} %get-tuple-element.5, pred[32,2,2048]{2,1,0:T(4,128)(4,1)S(1)} %broadcast_compare_fusion), kind=kLoop, calls=%fused_computation.6 | loop fusion | flops 33550336 | bytes 33718272 | tf_op jit(solution)/shard_map/reduce_sum | solution.py:30
  111.7 0.1 copy.23
  111.8 0.7 reshape.89
  112.6 3.3 %all-to-all-start = ((f32[4,1,1024]{2,1,0:T(1,128)}), f32[4,1,1024]{2,1,0:T(1,128)S(1)}, u32[]{:S(2)}, u32[]{:S(2)}) async-start(f32[4,1,1024]{2,1,0:T(1,128)} %reshape.89), calls=%async_computation | async-start | bytes 32768 | tf_op jit(solution)/shard_map/all_to_all | solution.py:35
  115.8 34.7 %divide_convert_fusion = bf16[32,2,64,512]{3,2,1,0:T(8,128)(2,1)} fusion(bf16[32,2048,576]{2,1,0:T(8,128)(2,1)} %bitcast, f32[32,2,64,2048]{3,2,1,0:T(8,128)} %get-tuple-element.6, f32[32,2,64]{2,1,0:T(2,128)S(1)} %get-tuple-element.5, pred[32,2,2048]{2,1,0:T(4,128)(4,1)S(1)} %broadcast_compare_fusion, f32[32,2,64]{2,1,0:T(2,128)S(1)} %fusion.3), kind=kOutput, calls=%fused_computation.13 | convolution fusion | flops 8627683328 | bytes 105021440 | tf_op jit(solution)/shard_map/bths,bsc->bthc/dot_general | solution.py:31
  150.6 8.4 %copy.26 = bf16[32,2,64,512]{3,1,0,2:T(2,128)(2,1)} copy(bf16[32,2,64,512]{3,2,1,0:T(8,128)(2,1)} %divide_convert_fusion) | data formatting | bytes 8388608 | tf_op jit(solution)/shard_map/convert_element_type | solution.py:32
  159.0 0.0 all-to-all-done
  159.0 5.0 %all-to-all-start.1 = ((bf16[32,2,64,512]{3,1,0,2:T(2,128)(2,1)}), bf16[32,2,64,512]{3,1,0,2:T(2,128)(2,1)}, u32[]{:S(2)}, u32[]{:S(2)}) async-start(bf16[32,2,64,512]{3,1,0,2:T(2,128)(2,1)} %copy.26), calls=%async_computation.1 | async-start | bytes 8388608 | tf_op jit(solution)/shard_map/all_to_all | solution.py:34
  164.0 0.5 broadcast.65
  164.5 0.7 reduce
  165.2 0.1 reshape.90
  165.5 0.5 copy.25
  165.9 45.9 %all-to-all-done.1 = bf16[32,2,64,512]{3,1,0,2:T(2,128)(2,1)} async-done(((bf16[32,2,64,512]{3,1,0,2:T(2,128)(2,1)}), bf16[32,2,64,512]{3,1,0,2:T(2,128)(2,1)}, u32[]{:S(2)}, u32[]{:S(2)}) %all-to-all-start.1) | async-done | bytes 4194336 | tf_op jit(solution)/shard_map/all_to_all | solution.py:34
  211.9 8.6 %fusion.9 = bf16[32,2,16,512]{3,1,0,2:T(2,128)(2,1)S(1)} fusion(bf16[32,2,4,16,512]{4,1,0,3,2:T(2,128)(2,1)} %bitcast.9, f32[32,2,4,16]{1,0,3,2:T(8,128)S(1)} %copy.25), kind=kLoop, calls=%fused_computation.12 | loop fusion | flops 5767168 | bytes 5259264 | tf_op jit(solution)/shard_map/reduce_sum | solution.py:38
  220.5 1.8 copy.27
  (8 shorter events, 0.1 us)
Async XLA Ops:
  6.5 43.7 %all-gather.2.cloned.1.call-start = ((), (), s32[]{:S(2)}) async-start(), calls=%async_computation.2 | async-start | bytes 6553600 | tf_op jit(solution)/shard_map/all_gather | solution.py:21
  112.6 46.4 %all-to-all-start = ((f32[4,1,1024]{2,1,0:T(1,128)}), f32[4,1,1024]{2,1,0:T(1,128)S(1)}, u32[]{:S(2)}, u32[]{:S(2)}) async-start(f32[4,1,1024]{2,1,0:T(1,128)} %reshape.89), calls=%async_computation | async-start | bytes 32768 | tf_op jit(solution)/shard_map/all_to_all | solution.py:35
  159.0 52.9 %all-to-all-start.1 = ((bf16[32,2,64,512]{3,1,0,2:T(2,128)(2,1)}), bf16[32,2,64,512]{3,1,0,2:T(2,128)(2,1)}, u32[]{:S(2)}, u32[]{:S(2)}) async-start(bf16[32,2,64,512]{3,1,0,2:T(2,128)(2,1)} %copy.26), calls=%async_computation.1 | async-start | bytes 8388608 | tf_op jit(solution)/shard_map/all_to_all | solution.py:34
Sparse Core Ops, SparseCore 0:
  8.9 41.2 all-gather.1
where the time goes:
time: 230 us; the launch traced here: 229 us
  waiting for transfers between devices  88.3 us (38%)
  matrix products  81.2 us (35%)
  other arithmetic  25.6 us (11%)
  between operations  13.5 us (6%)
  local copies, waits for them, and re-layouts  12.3 us (5%)
  starting transfers between devices  8.28 us (4%)
    dot_general x1, matrix products, local_step(): jnp.einsum('bthd,bsd->bths', q_all, local_keys, preferred_element_type=jn...  46.5 us
    all_to_all x1, waiting for transfers between devices, local_step(): lax.all_to_all(part_out, 'dcp', 2, 2, tiled=True)  45.9 us
    all_gather x1, waiting for transfers between devices, local_step(): q_all = lax.all_gather(q_blk, 'dcp', axis=2, tiled=True)  41.7 us
    dot_general x1, matrix products, local_step(): jnp.einsum('bths,bsc->bthc', weights.astype(jnp.bfloat16), local_keys[:,...  34.7 us
    reduce_sum x1, other arithmetic, local_step(): row_sum = jnp.sum(weights, axis=-1)  15 us
    reduce_sum x1, other arithmetic, local_step(): merged = jnp.sum(merge_w[..., None] * recv_out.astype(jnp.float32), axis=2)  8.61 us
    convert_element_type x1, local copies, waits for them, and re-layouts, local_step(): part_out = (part_out / row_sum[..., None]).astype(jnp.bfloat16)  8.43 us
    all_to_all x1, starting transfers between devices, local_step(): lax.all_to_all(part_out, 'dcp', 2, 2, tiled=True)  5.02 us
  transfers between devices with their start and end apart: 3, of which 2 were waited for; matrix products, arithmetic and copies ran while one was open for 20% of the time, Pallas kernels for 0%

commit v1 on v0

v1 whole, which is shorter than its diff:
```python
import functools

import jax
import jax.numpy as jnp
from jax import lax
from jax.experimental import pallas as pl
from jax.experimental.pallas import tpu as pltpu
from jax.sharding import PartitionSpec as P

LATENT = 512
ROPE = 64
NOPE = 128
PAGE = 64
BF = jnp.bfloat16
F32 = jnp.float32
MESH = pl.DeviceIdType.MESH

KV_SLOTS = 8
SCALE2 = (NOPE + ROPE) ** -0.5 * 1.4426950408889634
ROWS = 256
NT = (((1,), (1,)), ((), ()))


def kernel(batch, q_hbm, kv_hbm, len_ref, o_ref, kvb, stage, qx, qp, qd, rx, ro, rp, rd, s0, s1, m0, m1, p0, p1,
           ko, so, to, kl, sl, tl, co, cl, cr, cq, fc, fl, kv_sem, st_sem, x_ss, x_rs, f_ss, f_rs, p_ss, p_rs,
           o_ss, o_rs, c_ss, c_rs):
    pairs = batch // 2
    dummy = pairs + 2
    dp = lax.axis_index("dp")
    me = lax.axis_index("dcp")
    core = lax.rem(me, 2)
    peer = me + 1 - 2 * core
    cross = lax.rem(me + 2, 4)
    s_sc, m_sc, p_sc = (s0, s1), (m0, m1), (p0, p1)

    def kv_copy(b):
        slot = lax.rem(b, KV_SLOTS)
        return pltpu.make_async_copy(kv_hbm.at[b, :, 0], kvb.at[slot], kv_sem.at[slot])

    def remote(src, dst, ss, rs, target):
        return pltpu.make_async_remote_copy(src_ref=src, dst_ref=dst, send_sem=ss, recv_sem=rs,
                                            device_id=(dp, target), device_id_type=MESH)

    def piece(k, single):
        return (pl.ds(0, 1) if k == 0 else pl.ds(batch - 1, 1)) if single else pl.ds(2 * k - 1, 2)

    def q_cross(k, single=False):
        r = piece(k, single)
        return (remote(q_hbm.at[r, :, :, 0:LATENT], qx.at[r], x_ss.at[0, k], x_rs.at[0, k], cross),
                remote(ro.at[r], rx.at[r], x_ss.at[1, k], x_rs.at[1, k], cross))

    def q_forward(k, single=False):
        r = piece(k, single)
        return (remote(qx.at[r], qd.at[r], f_ss.at[0, k], f_rs.at[0, k], peer),
                remote(rx.at[r], rd.at[r], f_ss.at[1, k], f_rs.at[1, k], peer))

    def q_peer(k):
        r = pl.ds(0, 1) if k == 0 else pl.ds(1, batch - 1)
        return (remote(q_hbm.at[r, :, :, 0:LATENT], qp.at[r], p_ss.at[0, k], p_rs.at[0, k], peer),
                remote(ro.at[r], rp.at[r], p_ss.at[1, k], p_rs.at[1, k], peer))

    def o_peer(i):
        return (remote(so.at[i], to.at[i], o_ss.at[0, i], o_rs.at[0, i], peer),
                remote(sl.at[i], tl.at[i], o_ss.at[1, i], o_rs.at[1, i], peer))

    def o_cross(i):
        return (remote(co.at[i], cr.at[i], c_ss.at[0, i], c_rs.at[0, i], cross),
                remote(cl.at[i], cq.at[i], c_ss.at[1, i], c_rs.at[1, i], cross))

    stage_first = pltpu.make_async_copy(q_hbm.at[pl.ds(0, 1)], stage.at[pl.ds(0, 1)], st_sem.at[0])
    stage_rest = pltpu.make_async_copy(q_hbm.at[pl.ds(1, batch - 1)], stage.at[pl.ds(1, batch - 1)], st_sem.at[1])
    stage_first.start()
    stage_rest.start()
    for b in range(3):
        kv_copy(b).start()

    barrier = pltpu.get_barrier_semaphore()
    for other in (peer, cross):
        pl.semaphore_signal(barrier, inc=1, device_id=(dp, other), device_id_type=MESH)
    pl.semaphore_wait(barrier, 2)

    q_cross(0, True)[0].start()
    q_peer(0)[0].start()
    q_cross(1)[0].start()
    q_peer(1)[0].start()
    stage_first.wait()

    def pack(b, c):
        both = stage[b, :, :, LATENT:LATENT + ROPE]
        ro[b] = jnp.concatenate([both[0], both[1]], axis=1)
        return c

    pack(0, 0)
    stage_rest.wait()
    q_cross(0, True)[1].start()
    q_peer(0)[1].start()
    lax.fori_loop(1, batch, pack, 0)
    for b in range(3, 5):
        kv_copy(b).start()

    def start_rest(k, c):
        q_cross(k)[0].start()
        q_cross(k)[1].start()
        return c

    q_cross(1)[1].start()
    lax.fori_loop(2, pairs, start_rest, 0)
    for d in q_cross(pairs, True):
        d.start()
    q_peer(1)[1].start()

    lane = lax.broadcasted_iota(jnp.int32, (1, 128), 1)
    token = lax.rem(lane // 16, 2)
    sub = lax.broadcasted_iota(jnp.int32, (PAGE, 1), 0)
    pages = ROWS // PAGE

    def weights(b):
        def cols(lo):
            return jnp.concatenate([r[b, :, :, lo:lo + 256].reshape(32, 256) for r in (stage, qx, qp, qd)], 0)

        qa, qb = cols(0), cols(256)
        packed = [r[b] for r in (ro, rx, rp, rd)]
        qr = jnp.concatenate([x[:, lo:lo + ROPE] for x in packed for lo in (0, ROPE)], 0)
        z = jnp.zeros((128, 256), BF)
        z2 = jnp.zeros((128, ROPE), BF)
        last = jnp.concatenate([jnp.concatenate([qr, z2], 1), jnp.concatenate([z2, qr], 1)], 0)
        return jnp.concatenate([jnp.concatenate([qa, z], 0), jnp.concatenate([qb, z], 0), jnp.concatenate([z, qa], 0),
                                jnp.concatenate([z, qb], 0), last], 1)

    def keys(b, lo):
        slot = lax.rem(b, KV_SLOTS)
        halves = [kvb[slot, f:f + pages].reshape(ROWS, LATENT + ROPE) for f in (lo, lo + 16)]
        return jnp.concatenate([h[:, :LATENT] for h in halves] + [h[:, LATENT:] for h in halves], 1)

    def scores(b, par):
        w = weights(b)
        top = None
        last_pos = len_ref[b] - 2 + token
        for lo in range(0, 16, pages):
            s = lax.dot_general(keys(b, lo), w, NT, preferred_element_type=F32) * SCALE2
            for h in range(2):
                for g in range(pages):
                    t = s[g * PAGE:(g + 1) * PAGE, h * 128:(h + 1) * 128]
                    page = lo + 16 * h + g
                    if page >= 15:
                        pos = (page * 4 + me) * PAGE + sub
                        t = jnp.where(pos <= last_pos, t, -jnp.inf)
                    s_sc[par][page * PAGE:(page + 1) * PAGE, :] = t
                    for r in range(PAGE // 8):
                        v = t[r * 8:(r + 1) * 8]
                        top = v if top is None else jnp.maximum(top, v)
        m_sc[par][...] = top

    def softmax(par):
        m = jnp.max(m_sc[par][...], axis=0, keepdims=True)
        total = None
        for blk in range(16):
            p = jnp.exp2(s_sc[par][blk * 128:(blk + 1) * 128, :] - m)
            for r in range(16):
                v = p[r * 8:(r + 1) * 8]
                total = v if total is None else total + v
            p_sc[par][blk] = p.astype(BF).T
        return m, jnp.sum(total, axis=0, keepdims=True)

    def values(b, par):
        p = jnp.concatenate([p_sc[par][blk] for blk in range(16)], 1)
        v = kvb[lax.rem(b, KV_SLOTS), :, :, 0:LATENT].reshape(2048, LATENT)
        return jnp.dot(p, v, preferred_element_type=F32)

    def finish(i, par, m, total, acc):
        col = jnp.broadcast_to(1.0 / total, (128, 128)).T
        o = (acc * jnp.concatenate([col] * 4, 1)).astype(BF)
        ko[i, par] = o[0:64]
        so[i, par] = o[64:128]
        lse = m + jnp.log2(total)
        kl[i, par:par + 1, :] = lse
        sl[i, par:par + 1, :] = lse

    def combine(i, par):
        l1 = kl[i, par:par + 1, :]
        l2 = tl[i, par:par + 1, :]
        l2 = jnp.concatenate([l2[:, 64:], l2[:, :64]], 1)
        top = jnp.maximum(l1, l2)
        e1, e2 = jnp.exp2(l1 - top), jnp.exp2(l2 - top)
        den = e1 + e2
        w1, w2 = e1 / den, e2 / den
        col = jnp.broadcast_to(jnp.concatenate([w1[:, :64], w2[:, :64]], 1), (128, 128)).T
        c1 = jnp.concatenate([col[:64]] * 4, 1)
        c2 = jnp.concatenate([col[64:]] * 4, 1)
        merged = c1 * ko[i, par].astype(F32) + c2 * to[i, par].astype(F32)
        fc[i, par] = merged[:32]
        co[i, par] = merged[32:].astype(BF)
        lse = top + jnp.log2(den)
        fl[i, par:par + 1, :] = lse
        cl[i, par:par + 1, :] = lse

    for d in q_cross(0, True):
        d.wait_recv()
    for d in q_forward(0, True):
        d.start()
    for d in q_peer(0):
        d.wait_recv()
    kv_copy(0).wait()
    for d in q_forward(0, True):
        d.wait_recv()
    scores(0, 0)
    for d in q_cross(1):
        d.wait_recv()
    for d in q_forward(1):
        d.start()
    for d in q_peer(1):
        d.wait_recv()

    def block(i, final=False):
        a = 2 * i
        done = lax.rem(i + pairs, dummy)
        m, total = softmax(0)
        scores(a + 1, 1)
        finish(i, 0, m, total, values(a, 0))
        combine(done, 0)
        m, total = softmax(1)
        if not final:
            scores(a + 2, 0)
        finish(i, 1, m, total, values(a + 1, 1))
        combine(done, 1)

    def exchange(i):
        @pl.when(i >= 1)
        def _():
            for d in o_peer(i - 1):
                d.start()

        @pl.when(i >= 3)
        def _():
            for d in o_cross(i - 3):
                d.start()

        @pl.when(i >= 2)
        def _():
            for d in o_peer(i - 2):
                d.wait_recv()

    def body(i, c):
        for u in (1, 2):
            kv_copy(2 * i + u).wait()

        @pl.when(2 * i + 6 < batch)
        def _():
            for u in (5, 6):
                kv_copy(2 * i + u).start()

        @pl.when(2 * i + 6 == batch)
        def _():
            kv_copy(batch - 1).start()

        exchange(i)

        @pl.when(i + 2 < pairs)
        def _():
            for d in q_cross(i + 2):
                d.wait_recv()
            for d in q_forward(i + 2):
                d.start()

        @pl.when(i + 2 == pairs)
        def _():
            for d in q_cross(pairs, True):
                d.wait_recv()
            for d in q_forward(pairs, True):
                d.start()

        for d in q_forward(i + 1):
            d.wait_recv()
        block(i)
        return c

    lax.fori_loop(0, pairs - 1, body, 0)
    i = pairs - 1
    kv_copy(batch - 1).wait()
    exchange(i)
    for d in q_forward(pairs, True):
        d.wait_recv()
    block(i, True)
    for d in o_peer(i):
        d.start()
    for d in o_cross(i - 2):
        d.start()
    for j in (i - 1, i):
        for d in o_peer(j):
            d.wait_recv()
        for par in range(2):
            combine(j, par)
        for d in o_cross(j):
            d.start()

    def final(i, c):
        for d in o_cross(i):
            d.wait_recv()
        l1 = fl[i]
        l2 = cq[i]
        l2 = jnp.concatenate([l2[:, 32:], l2[:, :32]], 1)
        top = jnp.maximum(l1, l2)
        e1, e2 = jnp.exp2(l1 - top), jnp.exp2(l2 - top)
        den = e1 + e2
        w1, w2 = e1 / den, e2 / den
        row = jnp.concatenate([w1[0:1, :32], w2[0:1, :32], w1[1:2, :32], w2[1:2, :32]], 1)
        col = jnp.broadcast_to(row, (128, 128)).T
        for par in range(2):
            c1 = jnp.concatenate([col[64 * par:64 * par + 32]] * 4, 1)
            c2 = jnp.concatenate([col[64 * par + 32:64 * par + 64]] * 4, 1)
            o = (c1 * fc[i, par] + c2 * cr[i, par].astype(F32)).astype(BF)
            o_ref[2 * i + par] = o.reshape(2, 16, LATENT)
        return c

    lax.fori_loop(0, pairs, final, 0)

    def drain(k, c):
        for d in (*o_peer(k), *o_cross(k)):
            d.wait_send()
        return c

    lax.fori_loop(0, pairs, drain, 0)

    def drain_q(k, c):
        for d in (*q_cross(k), *q_forward(k)):
            d.wait_send()
        return c

    lax.fori_loop(1, pairs, drain_q, 0)
    for k in (0, pairs):
        for d in (*q_cross(k, True), *q_forward(k, True)):
            d.wait_send()
    for k in range(2):
        for d in q_peer(k):
            d.wait_send()


def solution(mesh):
    def local_step(q_blk, kv_blk, len_blk):
        batch, toks, heads, width = q_blk.shape
        pairs = batch // 2
        n = pairs + 2
        vm = pltpu.VMEM
        q_shape = (batch, toks, heads, LATENT)
        rope_shape = (batch, heads, toks * ROPE)
        dma = pltpu.SemaphoreType.DMA
        return pl.pallas_call(
            functools.partial(kernel, batch),
            out_shape=jax.ShapeDtypeStruct(q_shape, BF),
            in_specs=[pl.BlockSpec(memory_space=pl.ANY), pl.BlockSpec(memory_space=pl.ANY),
                      pl.BlockSpec(memory_space=pltpu.SMEM)],
            out_specs=pl.BlockSpec(memory_space=pltpu.VMEM),
            scratch_shapes=[
                vm((KV_SLOTS, kv_blk.shape[1], PAGE, width), BF),
                vm((batch, toks, heads, width), BF), vm(q_shape, BF), vm(q_shape, BF), vm(q_shape, BF),
                vm(rope_shape, BF), vm(rope_shape, BF), vm(rope_shape, BF), vm(rope_shape, BF),
                vm((2048, 128), F32), vm((2048, 128), F32), vm((8, 128), F32), vm((8, 128), F32),
                vm((16, 128, 128), BF), vm((16, 128, 128), BF),
                vm((n, 2, 64, LATENT), BF), vm((n, 2, 64, LATENT), BF), vm((n, 2, 64, LATENT), BF),
                vm((n, 2, 128), F32), vm((n, 2, 128), F32), vm((n, 2, 128), F32),
                vm((n, 2, 32, LATENT), BF), vm((n, 2, 128), F32), vm((n, 2, 32, LATENT), BF), vm((n, 2, 128), F32),
                vm((n, 2, 32, LATENT), F32), vm((n, 2, 128), F32),
                dma((KV_SLOTS,)), dma((2,)),
                dma((2, pairs + 1)), dma((2, pairs + 1)), dma((2, pairs + 1)), dma((2, pairs + 1)),
                dma((2, 2)), dma((2, 2)),
                dma((2, pairs)), dma((2, pairs)), dma((2, pairs)), dma((2, pairs)),
            ],
            compiler_params=pltpu.CompilerParams(collective_id=0, has_side_effects=True, vmem_limit_bytes=60 << 20),
        )(q_blk, kv_blk, len_blk)

    return jax.shard_map(local_step, mesh=mesh, in_specs=(P('dp', None, 'dcp', None), P('dp', None, 'dcp', None, None), P('dp')),
                         out_specs=P('dp', None, 'dcp', None), check_vma=False)
```

time: 230 us -> 62.2 us (0.27)
  waiting for transfers between devices: 88.3 us -> 0 us
  matrix products: 81.2 us -> 0 us
  Pallas kernels: 0 us -> 59.7 us
  other arithmetic: 25.6 us -> 0 us
  between operations: 13.5 us -> 0.01 us
  local copies, waits for them, and re-layouts: 12.3 us -> 2.31 us
  starting transfers between devices: 8.28 us -> 0 us
    dot_general x2 -> x0, matrix products: 81.2 us -> none  [the longest x1 46.5 us: local_step(): jnp.einsum('bthd,bsd->bths', q_all, local_keys, preferred_element_type=jn...]
    pallas_call x0 -> x1, Pallas kernels: none -> 59.7 us  [local_step(): pl.pallas_call(functools.partial(kernel, batch), out_shape=jax.ShapeDtype...]
    all_to_all x2 -> x0, waiting for transfers between devices: 45.9 us -> none  [the longest x1 45.9 us: local_step(): lax.all_to_all(part_out, 'dcp', 2, 2, tiled=True)]
    all_gather x1 -> x0, waiting for transfers between devices: 41.7 us -> none  [local_step(): q_all = lax.all_gather(q_blk, 'dcp', axis=2, tiled=True)]
    reduce_sum x3 -> x0, other arithmetic: 23.7 us -> none  [the longest x1 15 us: local_step(): row_sum = jnp.sum(weights, axis=-1)]
    convert_element_type x2 -> x0, local copies, waits for them, and re-layouts: 10.3 us -> none  [the longest x1 8.43 us: local_step(): part_out = (part_out / row_sum[..., None]).astype(jnp.bfloat16)]
    all_to_all x2 -> x0, starting transfers between devices: 8.28 us -> none  [the longest x1 5.02 us: local_step(): lax.all_to_all(part_out, 'dcp', 2, 2, tiled=True)]
  transfers between devices with their start and end apart: 3 -> 0, of which waited for: 2 -> 0; matrix products, arithmetic and copies ran while one was open for 20% -> 0% of each run, Pallas kernels for 0% -> 0%
where the time goes in v1:
time: 62.2 us; the launch traced here: 62 us
  Pallas kernels  59.7 us (96%)
  local copies, waits for them, and re-layouts  2.31 us (4%)
    pallas_call x1, Pallas kernels, local_step(): pl.pallas_call(functools.partial(kernel, batch), out_shape=jax.ShapeDtype...  59.7 us
    unnamed x1, local copies, waits for them, and re-layouts  2.31 us

profile of v1, /device:TPU:0, one launch (start us, length us, event | category | flops | bytes accessed | tf_op | source)
XLA Modules:
  0.0 62.0 jit_solution(6319066421822541743)
XLA Ops:
  0.0 59.7 %shard_map.37 = bf16[32,2,16,512]{3,2,1,0:T(8,128)(2,1)} custom-call(bf16[32,2,16,576]{3,2,1,0:T(8,128)(2,1)} %q_hbm.1, bf16[32,32,1,64,576]{4,3,2,1,0:T(8,128)(2,1)} %kv_hbm.1, s32[32]{0:T(128)} %len_ref.1), custom_call_target="tpu_custom_call" | custom-call | tf_op jit(solution)/shard_map/pallas_call | solution.py:347
  59.7 2.3 %copy.5 = bf16[32,2,16,512]{3,2,1,0:T(8,128)(2,1)} copy(bf16[32,2,16,512]{3,2,1,0:T(8,128)(2,1)} %shard_map.37) | data formatting | bytes 2097152

commit v2 on v1

--- a/solution.py
+++ b/solution.py
@@ -46,7 +46,7 @@
 
     def q_cross(k, single=False):
         r = piece(k, single)
-        return (remote(q_hbm.at[r, :, :, 0:LATENT], qx.at[r], x_ss.at[0, k], x_rs.at[0, k], cross),
+        return (remote((stage if single and k == 0 else q_hbm).at[r, :, :, 0:LATENT], qx.at[r], x_ss.at[0, k], x_rs.at[0, k], cross),
                 remote(ro.at[r], rx.at[r], x_ss.at[1, k], x_rs.at[1, k], cross))
 
     def q_forward(k, single=False):
@@ -56,7 +56,7 @@
 
     def q_peer(k):
         r = pl.ds(0, 1) if k == 0 else pl.ds(1, batch - 1)
-        return (remote(q_hbm.at[r, :, :, 0:LATENT], qp.at[r], p_ss.at[0, k], p_rs.at[0, k], peer),
+        return (remote((stage if k == 0 else q_hbm).at[r, :, :, 0:LATENT], qp.at[r], p_ss.at[0, k], p_rs.at[0, k], peer),
                 remote(ro.at[r], rp.at[r], p_ss.at[1, k], p_rs.at[1, k], peer))
 
     def o_peer(i):
@@ -71,43 +71,42 @@
     stage_rest = pltpu.make_async_copy(q_hbm.at[pl.ds(1, batch - 1)], stage.at[pl.ds(1, batch - 1)], st_sem.at[1])
     stage_first.start()
     stage_rest.start()
-    for b in range(3):
-        kv_copy(b).start()
+
+    def pack(b, c):
+        both = stage[b, :, :, LATENT:LATENT + ROPE]
+        ro[b] = jnp.concatenate([both[0], both[1]], axis=1)
+        return c
 
     barrier = pltpu.get_barrier_semaphore()
     for other in (peer, cross):
         pl.semaphore_signal(barrier, inc=1, device_id=(dp, other), device_id_type=MESH)
+    stage_first.wait()
+    pack(0, 0)
     pl.semaphore_wait(barrier, 2)
 
-    q_cross(0, True)[0].start()
-    q_peer(0)[0].start()
+    for d in (*q_cross(0, True), *q_peer(0)):
+        d.start()
     q_cross(1)[0].start()
     q_peer(1)[0].start()
-    stage_first.wait()
-
-    def pack(b, c):
-        both = stage[b, :, :, LATENT:LATENT + ROPE]
-        ro[b] = jnp.concatenate([both[0], both[1]], axis=1)
-        return c
-
-    pack(0, 0)
+    q_cross(2)[0].start()
+    for b in range(3):
+        kv_copy(b).start()
     stage_rest.wait()
-    q_cross(0, True)[1].start()
-    q_peer(0)[1].start()
     lax.fori_loop(1, batch, pack, 0)
+    q_peer(1)[1].start()
+    q_cross(1)[1].start()
+    q_cross(2)[1].start()
+
+    def start_rest(k, c):
+        for d in q_cross(k):
+            d.start()
+        return c
+
+    lax.fori_loop(3, pairs, start_rest, 0)
+    for d in q_cross(pairs, True):
+        d.start()
     for b in range(3, 5):
         kv_copy(b).start()
-
-    def start_rest(k, c):
-        q_cross(k)[0].start()
-        q_cross(k)[1].start()
-        return c
-
-    q_cross(1)[1].start()
-    lax.fori_loop(2, pairs, start_rest, 0)
-    for d in q_cross(pairs, True):
-        d.start()
-    q_peer(1)[1].start()
 
     lane = lax.broadcasted_iota(jnp.int32, (1, 128), 1)
     token = lax.rem(lane // 16, 2)
@@ -347,7 +346,7 @@
         return pl.pallas_call(
             functools.partial(kernel, batch),
             out_shape=jax.ShapeDtypeStruct(q_shape, BF),
-            in_specs=[pl.BlockSpec(memory_space=pl.ANY), pl.BlockSpec(memory_space=pl.ANY),
+            in_specs=[pl.BlockSpec(memory_space=pltpu.HBM), pl.BlockSpec(memory_space=pltpu.HBM),
                       pl.BlockSpec(memory_space=pltpu.SMEM)],
             out_specs=pl.BlockSpec(memory_space=pltpu.VMEM),
             scratch_shapes=[
@@ -365,7 +364,7 @@
                 dma((2, 2)), dma((2, 2)),
                 dma((2, pairs)), dma((2, pairs)), dma((2, pairs)), dma((2, pairs)),
             ],
-            compiler_params=pltpu.CompilerParams(collective_id=0, has_side_effects=True, vmem_limit_bytes=60 << 20),
+            compiler_params=pltpu.CompilerParams(collective_id=0, has_side_effects=True, vmem_limit_bytes=55_000_000),
         )(q_blk, kv_blk, len_blk)
 
     return jax.shard_map(local_step, mesh=mesh, in_specs=(P('dp', None, 'dcp', None), P('dp', None, 'dcp', None, None), P('dp')),

time: 62.2 us -> 58.4 us (0.939)
  Pallas kernels: 59.7 us -> 56.6 us
  local copies, waits for them, and re-layouts: 2.31 us -> 1.63 us
    pallas_call x1, Pallas kernels: 59.7 us -> 56.6 us  [local_step(): pl.pallas_call(functools.partial(kernel, batch), out_shape=jax.ShapeDtype...]
    unnamed x1 -> x3, local copies, waits for them, and re-layouts: 2.31 us -> 1.63 us
where the time goes in v2:
time: 58.4 us; the launch traced here: 58.2 us
  Pallas kernels  56.6 us (97%)
  local copies, waits for them, and re-layouts  1.63 us (3%)
    pallas_call x1, Pallas kernels, local_step(): pl.pallas_call(functools.partial(kernel, batch), out_shape=jax.ShapeDtype...  56.6 us
    unnamed x3, local copies, waits for them, and re-layouts  1.63 us

profile of v2, /device:TPU:0, one launch (start us, length us, event | category | flops | bytes accessed | tf_op | source)
XLA Modules:
  0.0 58.2 jit_solution(8188733549046729432)
XLA Ops:
  0.0 0.0 copy-start
  0.0 0.7 %copy-done = s32[32]{0:T(128)S(1)} copy-done((s32[32]{0:T(128)S(1)}, s32[32]{0:T(128)}, u32[]{:S(2)}) %copy-start) | copy-done | bytes 152
  0.7 56.6 %shard_map.37 = bf16[32,2,16,512]{3,2,1,0:T(8,128)(2,1)S(1)} custom-call(bf16[32,2,16,576]{3,2,1,0:T(8,128)(2,1)} %q_hbm.1, bf16[32,32,1,64,576]{4,3,2,1,0:T(8,128)(2,1)} %kv_hbm.1, s32[32]{0:T(128)S(1)} %copy-done), custom_call_target="tpu_custom_call" | custom-call | tf_op jit(solution)/shard_map/pallas_call | solution.py:346
  57.3 1.0 %copy.5 = bf16[32,2,16,512]{3,2,1,0:T(8,128)(2,1)} copy(bf16[32,2,16,512]{3,2,1,0:T(8,128)(2,1)S(1)} %shard_map.37) | data formatting | bytes 2097152
Async XLA Ops:
  0.0 0.7 %copy-start = (s32[32]{0:T(128)S(1)}, s32[32]{0:T(128)}, u32[]{:S(2)}) copy-start(s32[32]{0:T(128)} %len_ref.1) | copy-start | bytes 388

commit v3 on v2

--- a/solution.py
+++ b/solution.py
@@ -23,7 +23,7 @@
 
 def kernel(batch, q_hbm, kv_hbm, len_ref, o_ref, kvb, stage, qx, qp, qd, rx, ro, rp, rd, s0, s1, m0, m1, p0, p1,
            ko, so, to, kl, sl, tl, co, cl, cr, cq, fc, fl, kv_sem, st_sem, x_ss, x_rs, f_ss, f_rs, p_ss, p_rs,
-           o_ss, o_rs, c_ss, c_rs):
+           r_ss, r_rs, o_ss, o_rs, c_ss, c_rs, l_ss, l_rs):
     pairs = batch // 2
     dummy = pairs + 2
     dp = lax.axis_index("dp")
@@ -33,9 +33,16 @@
     cross = lax.rem(me + 2, 4)
     s_sc, m_sc, p_sc = (s0, s1), (m0, m1), (p0, p1)
 
-    def kv_copy(b):
-        slot = lax.rem(b, KV_SLOTS)
-        return pltpu.make_async_copy(kv_hbm.at[b, :, 0], kvb.at[slot], kv_sem.at[slot])
+    def kv_slot(b):
+        return lax.rem(b + 1, KV_SLOTS)
+
+    def kv_copy(k):
+        if isinstance(k, int) and k in (0, pairs):
+            b = 0 if k == 0 else batch - 1
+            slot = kv_slot(b)
+            return pltpu.make_async_copy(kv_hbm.at[b, :, 0], kvb.at[slot], kv_sem.at[slot // 2])
+        slot = kv_slot(2 * k - 1)
+        return pltpu.make_async_copy(kv_hbm.at[pl.ds(2 * k - 1, 2), :, 0], kvb.at[pl.ds(slot, 2)], kv_sem.at[slot // 2])
 
     def remote(src, dst, ss, rs, target):
         return pltpu.make_async_remote_copy(src_ref=src, dst_ref=dst, send_sem=ss, recv_sem=rs,
@@ -46,26 +53,41 @@
 
     def q_cross(k, single=False):
         r = piece(k, single)
-        return (remote((stage if single and k == 0 else q_hbm).at[r, :, :, 0:LATENT], qx.at[r], x_ss.at[0, k], x_rs.at[0, k], cross),
-                remote(ro.at[r], rx.at[r], x_ss.at[1, k], x_rs.at[1, k], cross))
+        return remote((stage if single and k == 0 else q_hbm).at[r, :, :, 0:LATENT], qx.at[r], x_ss.at[k], x_rs.at[k],
+                      cross)
 
     def q_forward(k, single=False):
         r = piece(k, single)
-        return (remote(qx.at[r], qd.at[r], f_ss.at[0, k], f_rs.at[0, k], peer),
-                remote(rx.at[r], rd.at[r], f_ss.at[1, k], f_rs.at[1, k], peer))
+        return remote(qx.at[r], qd.at[r], f_ss.at[k], f_rs.at[k], peer)
 
     def q_peer(k):
         r = pl.ds(0, 1) if k == 0 else pl.ds(1, batch - 1)
-        return (remote((stage if k == 0 else q_hbm).at[r, :, :, 0:LATENT], qp.at[r], p_ss.at[0, k], p_rs.at[0, k], peer),
-                remote(ro.at[r], rp.at[r], p_ss.at[1, k], p_rs.at[1, k], peer))
+        return remote((stage if k == 0 else q_hbm).at[r, :, :, 0:LATENT], qp.at[r], p_ss.at[k], p_rs.at[k], peer)
+
+    def rope(k, to_cross, relay):
+        r = (pl.ds(0, 1), pl.ds(1, 6), pl.ds(7, batch - 7))[k]
+        n = 3 * (0 if to_cross else 2 if relay else 1) + k
+        src, dst = (ro, rx) if to_cross else (rx, rd) if relay else (ro, rp)
+        return remote(src.at[r], dst.at[r], r_ss.at[n], r_rs.at[n], cross if to_cross else peer)
+
+    def rope_cross(k):
+        return rope(k, True, False)
+
+    def rope_peer(k):
+        return rope(k, False, False)
+
+    def rope_forward(k):
+        return rope(k, False, True)
 
     def o_peer(i):
         return (remote(so.at[i], to.at[i], o_ss.at[0, i], o_rs.at[0, i], peer),
                 remote(sl.at[i], tl.at[i], o_ss.at[1, i], o_rs.at[1, i], peer))
 
     def o_cross(i):
-        return (remote(co.at[i], cr.at[i], c_ss.at[0, i], c_rs.at[0, i], cross),
-                remote(cl.at[i], cq.at[i], c_ss.at[1, i], c_rs.at[1, i], cross))
+        return remote(co.at[i], cr.at[i], c_ss.at[i], c_rs.at[i], cross)
+
+    def lse_cross(g):
+        return remote(cl.at[2 * g + 1], cq.at[2 * g + 1], l_ss.at[g], l_rs.at[g], cross)
 
     stage_first = pltpu.make_async_copy(q_hbm.at[pl.ds(0, 1)], stage.at[pl.ds(0, 1)], st_sem.at[0])
     stage_rest = pltpu.make_async_copy(q_hbm.at[pl.ds(1, batch - 1)], stage.at[pl.ds(1, batch - 1)], st_sem.at[1])
@@ -84,29 +106,25 @@
     pack(0, 0)
     pl.semaphore_wait(barrier, 2)
 
-    for d in (*q_cross(0, True), *q_peer(0)):
-        d.start()
-    q_cross(1)[0].start()
-    q_peer(1)[0].start()
-    q_cross(2)[0].start()
-    for b in range(3):
-        kv_copy(b).start()
+    for d in (q_cross(0, True), rope_cross(0), q_peer(0), rope_peer(0), q_cross(1), q_peer(1)):
+        d.start()
+    for k in range(2):
+        kv_copy(k).start()
     stage_rest.wait()
-    lax.fori_loop(1, batch, pack, 0)
-    q_peer(1)[1].start()
-    q_cross(1)[1].start()
-    q_cross(2)[1].start()
+    lax.fori_loop(1, 7, pack, 0)
+    for d in (rope_cross(1), rope_peer(1), q_cross(2), q_cross(3)):
+        d.start()
+    lax.fori_loop(7, batch, pack, 0)
+    for d in (rope_peer(2), rope_cross(2)):
+        d.start()
 
     def start_rest(k, c):
-        for d in q_cross(k):
-            d.start()
-        return c
-
-    lax.fori_loop(3, pairs, start_rest, 0)
-    for d in q_cross(pairs, True):
-        d.start()
-    for b in range(3, 5):
-        kv_copy(b).start()
+        q_cross(k).start()
+        return c
+
+    lax.fori_loop(4, pairs, start_rest, 0)
+    q_cross(pairs, True).start()
+    kv_copy(2).start()
 
     lane = lax.broadcasted_iota(jnp.int32, (1, 128), 1)
     token = lax.rem(lane // 16, 2)
@@ -127,7 +145,7 @@
                                 jnp.concatenate([z, qb], 0), last], 1)
 
     def keys(b, lo):
-        slot = lax.rem(b, KV_SLOTS)
+        slot = kv_slot(b)
         halves = [kvb[slot, f:f + pages].reshape(ROWS, LATENT + ROPE) for f in (lo, lo + 16)]
         return jnp.concatenate([h[:, :LATENT] for h in halves] + [h[:, LATENT:] for h in halves], 1)
 
@@ -163,7 +181,7 @@
 
     def values(b, par):
         p = jnp.concatenate([p_sc[par][blk] for blk in range(16)], 1)
-        v = kvb[lax.rem(b, KV_SLOTS), :, :, 0:LATENT].reshape(2048, LATENT)
+        v = kvb[kv_slot(b), :, :, 0:LATENT].reshape(2048, LATENT)
         return jnp.dot(p, v, preferred_element_type=F32)
 
     def finish(i, par, m, total, acc):
@@ -191,24 +209,27 @@
         co[i, par] = merged[32:].astype(BF)
         lse = top + jnp.log2(den)
         fl[i, par:par + 1, :] = lse
-        cl[i, par:par + 1, :] = lse
-
-    for d in q_cross(0, True):
-        d.wait_recv()
-    for d in q_forward(0, True):
-        d.start()
-    for d in q_peer(0):
+        if par == 1:
+            before = lax.rem(i + dummy - 1, dummy)
+            cl[i] = jnp.concatenate([r[:, 32:64] for r in (fl[before, 0:1, :], fl[before, 1:2, :], fl[i, 0:1, :], lse)], 1)
+
+    for d in (q_cross(0, True), rope_cross(0)):
+        d.wait_recv()
+    for d in (q_forward(0, True), rope_forward(0)):
+        d.start()
+    for d in (q_peer(0), rope_peer(0)):
         d.wait_recv()
     kv_copy(0).wait()
-    for d in q_forward(0, True):
+    for d in (q_forward(0, True), rope_forward(0)):
         d.wait_recv()
     scores(0, 0)
-    for d in q_cross(1):
-        d.wait_recv()
-    for d in q_forward(1):
-        d.start()
-    for d in q_peer(1):
-        d.wait_recv()
+    for d in (q_cross(1), rope_cross(1)):
+        d.wait_recv()
+    for d in (q_forward(1), rope_forward(1)):
+        d.start()
+    for d in (q_peer(1), rope_peer(1), rope_peer(2)):
+        d.wait_recv()
+    rope_forward(1).wait_recv()
 
     def block(i, final=False):
         a = 2 * i
@@ -223,115 +244,103 @@
         finish(i, 1, m, total, values(a + 1, 1))
         combine(done, 1)
 
-    def exchange(i):
-        @pl.when(i >= 1)
-        def _():
+    def step(i):
+        static = isinstance(i, int)
+        single = static and i + 1 == pairs
+        kv_copy(i + 1).wait()
+        q_forward(i + 1, single).wait_recv()
+        if static and i == 3:
+            rope_forward(2).wait_recv()
+        if not static or i + 3 <= pairs:
+            kv_copy(i + 3).start()
+        if not static or i >= 1:
             for d in o_peer(i - 1):
                 d.start()
-
-        @pl.when(i >= 3)
-        def _():
-            for d in o_cross(i - 3):
-                d.start()
-
-        @pl.when(i >= 2)
-        def _():
+        if not static or i >= 3:
+            o_cross(i - 3).start()
+            if static and i % 2 == 0:
+                lse_cross((i - 4) // 2).start()
+            if not static:
+                @pl.when(lax.rem(i, 2) == 0)
+                def _():
+                    lse_cross((i - 4) // 2).start()
+        if not static or i + 2 <= pairs:
+            single = static and i + 2 == pairs
+            q_cross(i + 2, single).wait_recv()
+            q_forward(i + 2, single).start()
+        if static and i == 2:
+            rope_cross(2).wait_recv()
+            rope_forward(2).start()
+        if not static or i >= 2:
             for d in o_peer(i - 2):
                 d.wait_recv()
+        block(i, static and i == pairs - 1)
 
     def body(i, c):
-        for u in (1, 2):
-            kv_copy(2 * i + u).wait()
-
-        @pl.when(2 * i + 6 < batch)
-        def _():
-            for u in (5, 6):
-                kv_copy(2 * i + u).start()
-
-        @pl.when(2 * i + 6 == batch)
-        def _():
-            kv_copy(batch - 1).start()
-
-        exchange(i)
-
-        @pl.when(i + 2 < pairs)
-        def _():
-            for d in q_cross(i + 2):
-                d.wait_recv()
-            for d in q_forward(i + 2):
-                d.start()
-
-        @pl.when(i + 2 == pairs)
-        def _():
-            for d in q_cross(pairs, True):
-                d.wait_recv()
-            for d in q_forward(pairs, True):
-                d.start()
-
-        for d in q_forward(i + 1):
-            d.wait_recv()
-        block(i)
-        return c
-
-    lax.fori_loop(0, pairs - 1, body, 0)
+        step(i)
+        return c
+
+    for i in range(4):
+        step(i)
+    lax.fori_loop(4, pairs - 3, body, 0)
+    for i in range(pairs - 3, pairs):
+        step(i)
     i = pairs - 1
-    kv_copy(batch - 1).wait()
-    exchange(i)
-    for d in q_forward(pairs, True):
-        d.wait_recv()
-    block(i, True)
     for d in o_peer(i):
         d.start()
-    for d in o_cross(i - 2):
-        d.start()
+    o_cross(i - 2).start()
+    lse_cross((i - 3) // 2).start()
     for j in (i - 1, i):
         for d in o_peer(j):
             d.wait_recv()
         for par in range(2):
             combine(j, par)
-        for d in o_cross(j):
-            d.start()
-
-    def final(i, c):
-        for d in o_cross(i):
-            d.wait_recv()
-        l1 = fl[i]
-        l2 = cq[i]
-        l2 = jnp.concatenate([l2[:, 32:], l2[:, :32]], 1)
-        top = jnp.maximum(l1, l2)
-        e1, e2 = jnp.exp2(l1 - top), jnp.exp2(l2 - top)
-        den = e1 + e2
-        w1, w2 = e1 / den, e2 / den
-        row = jnp.concatenate([w1[0:1, :32], w2[0:1, :32], w1[1:2, :32], w2[1:2, :32]], 1)
-        col = jnp.broadcast_to(row, (128, 128)).T
-        for par in range(2):
-            c1 = jnp.concatenate([col[64 * par:64 * par + 32]] * 4, 1)
-            c2 = jnp.concatenate([col[64 * par + 32:64 * par + 64]] * 4, 1)
-            o = (c1 * fc[i, par] + c2 * cr[i, par].astype(F32)).astype(BF)
-            o_ref[2 * i + par] = o.reshape(2, 16, LATENT)
-        return c
-
-    lax.fori_loop(0, pairs, final, 0)
-
-    def drain(k, c):
-        for d in (*o_peer(k), *o_cross(k)):
-            d.wait_send()
-        return c
-
-    lax.fori_loop(0, pairs, drain, 0)
+        o_cross(j).start()
+    lse_cross((i - 1) // 2).start()
 
     def drain_q(k, c):
-        for d in (*q_cross(k), *q_forward(k)):
-            d.wait_send()
+        q_cross(k).wait_send()
+        q_forward(k).wait_send()
         return c
 
     lax.fori_loop(1, pairs, drain_q, 0)
     for k in (0, pairs):
-        for d in (*q_cross(k, True), *q_forward(k, True)):
+        q_cross(k, True).wait_send()
+        q_forward(k, True).wait_send()
+    for k in range(2):
+        q_peer(k).wait_send()
+    for k in range(3):
+        for d in (rope_cross(k), rope_peer(k), rope_forward(k)):
             d.wait_send()
-    for k in range(2):
-        for d in q_peer(k):
+
+    def drain_peer(k, c):
+        for d in o_peer(k):
             d.wait_send()
+        return c
+
+    lax.fori_loop(0, pairs, drain_peer, 0)
+
+    def final(g, c):
+        lse_cross(g).wait_recv()
+        for u in range(2):
+            i = 2 * g + u
+            o_cross(i).wait_recv()
+            l1 = jnp.concatenate([fl[i, 0:1, :32], fl[i, 1:2, :32]], 1)
+            l2 = cq[2 * g + 1][:, 64 * u:64 * u + 64]
+            top = jnp.maximum(l1, l2)
+            e1, e2 = jnp.exp2(l1 - top), jnp.exp2(l2 - top)
+            den = e1 + e2
+            col = jnp.broadcast_to(jnp.concatenate([e1 / den, e2 / den], 1), (128, 128)).T
+            for par in range(2):
+                c1 = jnp.concatenate([col[32 * par:32 * par + 32]] * 4, 1)
+                c2 = jnp.concatenate([col[64 + 32 * par:96 + 32 * par]] * 4, 1)
+                o = (c1 * fc[i, par] + c2 * cr[i, par].astype(F32)).astype(BF)
+                o_ref[2 * i + par] = o.reshape(2, 16, LATENT)
+            o_cross(i).wait_send()
+        lse_cross(g).wait_send()
+        return c
+
+    lax.fori_loop(0, pairs // 2, final, 0)
 
 
 def solution(mesh):
@@ -357,12 +366,12 @@
                 vm((16, 128, 128), BF), vm((16, 128, 128), BF),
                 vm((n, 2, 64, LATENT), BF), vm((n, 2, 64, LATENT), BF), vm((n, 2, 64, LATENT), BF),
                 vm((n, 2, 128), F32), vm((n, 2, 128), F32), vm((n, 2, 128), F32),
-                vm((n, 2, 32, LATENT), BF), vm((n, 2, 128), F32), vm((n, 2, 32, LATENT), BF), vm((n, 2, 128), F32),
+                vm((n, 2, 32, LATENT), BF), vm((n, 1, 128), F32), vm((n, 2, 32, LATENT), BF), vm((n, 1, 128), F32),
                 vm((n, 2, 32, LATENT), F32), vm((n, 2, 128), F32),
-                dma((KV_SLOTS,)), dma((2,)),
-                dma((2, pairs + 1)), dma((2, pairs + 1)), dma((2, pairs + 1)), dma((2, pairs + 1)),
-                dma((2, 2)), dma((2, 2)),
-                dma((2, pairs)), dma((2, pairs)), dma((2, pairs)), dma((2, pairs)),
+                dma((KV_SLOTS // 2,)), dma((2,)),
+                dma((pairs + 1,)), dma((pairs + 1,)), dma((pairs + 1,)), dma((pairs + 1,)), dma((2,)), dma((2,)),
+                dma((9,)), dma((9,)), dma((2, pairs)), dma((2, pairs)), dma((pairs,)), dma((pairs,)),
+                dma((pairs // 2,)), dma((pairs // 2,)),
             ],
             compiler_params=pltpu.CompilerParams(collective_id=0, has_side_effects=True, vmem_limit_bytes=55_000_000),
         )(q_blk, kv_blk, len_blk)

time: 58.4 us -> 57.6 us (0.986)
  Pallas kernels: 56.6 us -> 55.8 us
    pallas_call x1, Pallas kernels: 56.6 us -> 55.8 us  [local_step(): pl.pallas_call(functools.partial(kernel, batch), out_shape=jax.ShapeDtype...]
where the time goes in v3:
time: 57.6 us; the launch traced here: 57.4 us
  Pallas kernels  55.8 us (97%)
  local copies, waits for them, and re-layouts  1.63 us (3%)
    pallas_call x1, Pallas kernels, local_step(): pl.pallas_call(functools.partial(kernel, batch), out_shape=jax.ShapeDtype...  55.8 us
    unnamed x3, local copies, waits for them, and re-layouts  1.63 us

profile of v3, /device:TPU:0, one launch (start us, length us, event | category | flops | bytes accessed | tf_op | source)
XLA Modules:
  0.0 57.4 jit_solution(811410106215060207)
XLA Ops:
  0.0 0.0 copy-start
  0.0 0.7 %copy-done = s32[32]{0:T(128)S(1)} copy-done((s32[32]{0:T(128)S(1)}, s32[32]{0:T(128)}, u32[]{:S(2)}) %copy-start) | copy-done | bytes 152
  0.7 55.8 %shard_map.37 = bf16[32,2,16,512]{3,2,1,0:T(8,128)(2,1)S(1)} custom-call(bf16[32,2,16,576]{3,2,1,0:T(8,128)(2,1)} %q_hbm.1, bf16[32,32,1,64,576]{4,3,2,1,0:T(8,128)(2,1)} %kv_hbm.1, s32[32]{0:T(128)S(1)} %copy-done), custom_call_target="tpu_custom_call" | custom-call | tf_op jit(solution)/shard_map/pallas_call | solution.py:355
  56.5 1.0 %copy.5 = bf16[32,2,16,512]{3,2,1,0:T(8,128)(2,1)} copy(bf16[32,2,16,512]{3,2,1,0:T(8,128)(2,1)S(1)} %shard_map.37) | data formatting | bytes 2097152
Async XLA Ops:
  0.0 0.7 %copy-start = (s32[32]{0:T(128)S(1)}, s32[32]{0:T(128)}, u32[]{:S(2)}) copy-start(s32[32]{0:T(128)} %len_ref.1) | copy-start | bytes 388

commit v4 on v3

--- a/solution.py
+++ b/solution.py
@@ -21,7 +21,7 @@
 NT = (((1,), (1,)), ((), ()))
 
 
-def kernel(batch, q_hbm, kv_hbm, len_ref, o_ref, kvb, stage, qx, qp, qd, rx, ro, rp, rd, s0, s1, m0, m1, p0, p1,
+def kernel(batch, q_hbm, kv_hbm, len_hbm, o_ref, len_ref, kvb, stage, qx, qp, qd, rx, ro, rp, rd, s0, s1, m0, m1, p0, p1,
            ko, so, to, kl, sl, tl, co, cl, cr, cq, fc, fl, kv_sem, st_sem, x_ss, x_rs, f_ss, f_rs, p_ss, p_rs,
            r_ss, r_rs, o_ss, o_rs, c_ss, c_rs, l_ss, l_rs):
     pairs = batch // 2
@@ -53,7 +53,7 @@
 
     def q_cross(k, single=False):
         r = piece(k, single)
-        return remote((stage if single and k == 0 else q_hbm).at[r, :, :, 0:LATENT], qx.at[r], x_ss.at[k], x_rs.at[k],
+        return remote(q_hbm.at[r, :, :, 0:LATENT], qx.at[r], x_ss.at[k], x_rs.at[k],
                       cross)
 
     def q_forward(k, single=False):
@@ -62,7 +62,7 @@
 
     def q_peer(k):
         r = pl.ds(0, 1) if k == 0 else pl.ds(1, batch - 1)
-        return remote((stage if k == 0 else q_hbm).at[r, :, :, 0:LATENT], qp.at[r], p_ss.at[k], p_rs.at[k], peer)
+        return remote(q_hbm.at[r, :, :, 0:LATENT], qp.at[r], p_ss.at[k], p_rs.at[k], peer)
 
     def rope(k, to_cross, relay):
         r = (pl.ds(0, 1), pl.ds(1, 6), pl.ds(7, batch - 7))[k]
@@ -93,6 +93,8 @@
     stage_rest = pltpu.make_async_copy(q_hbm.at[pl.ds(1, batch - 1)], stage.at[pl.ds(1, batch - 1)], st_sem.at[1])
     stage_first.start()
     stage_rest.start()
+    len_copy = pltpu.make_async_copy(len_hbm, len_ref, st_sem.at[2])
+    len_copy.start()
 
     def pack(b, c):
         both = stage[b, :, :, LATENT:LATENT + ROPE]
@@ -102,11 +104,13 @@
     barrier = pltpu.get_barrier_semaphore()
     for other in (peer, cross):
         pl.semaphore_signal(barrier, inc=1, device_id=(dp, other), device_id_type=MESH)
+    pl.semaphore_wait(barrier, 2)
+
+    for d in (q_cross(0, True), q_peer(0)):
+        d.start()
     stage_first.wait()
     pack(0, 0)
-    pl.semaphore_wait(barrier, 2)
-
-    for d in (q_cross(0, True), rope_cross(0), q_peer(0), rope_peer(0), q_cross(1), q_peer(1)):
+    for d in (rope_cross(0), rope_peer(0), q_cross(1), q_peer(1)):
         d.start()
     for k in range(2):
         kv_copy(k).start()
@@ -220,6 +224,7 @@
     for d in (q_peer(0), rope_peer(0)):
         d.wait_recv()
     kv_copy(0).wait()
+    len_copy.wait()
     for d in (q_forward(0, True), rope_forward(0)):
         d.wait_recv()
     scores(0, 0)
@@ -356,9 +361,10 @@
             functools.partial(kernel, batch),
             out_shape=jax.ShapeDtypeStruct(q_shape, BF),
             in_specs=[pl.BlockSpec(memory_space=pltpu.HBM), pl.BlockSpec(memory_space=pltpu.HBM),
-                      pl.BlockSpec(memory_space=pltpu.SMEM)],
+                      pl.BlockSpec(memory_space=pltpu.HBM)],
             out_specs=pl.BlockSpec(memory_space=pltpu.VMEM),
             scratch_shapes=[
+                pltpu.SMEM((batch,), jnp.int32),
                 vm((KV_SLOTS, kv_blk.shape[1], PAGE, width), BF),
                 vm((batch, toks, heads, width), BF), vm(q_shape, BF), vm(q_shape, BF), vm(q_shape, BF),
                 vm(rope_shape, BF), vm(rope_shape, BF), vm(rope_shape, BF), vm(rope_shape, BF),
@@ -368,13 +374,13 @@
                 vm((n, 2, 128), F32), vm((n, 2, 128), F32), vm((n, 2, 128), F32),
                 vm((n, 2, 32, LATENT), BF), vm((n, 1, 128), F32), vm((n, 2, 32, LATENT), BF), vm((n, 1, 128), F32),
                 vm((n, 2, 32, LATENT), F32), vm((n, 2, 128), F32),
-                dma((KV_SLOTS // 2,)), dma((2,)),
+                dma((KV_SLOTS // 2,)), dma((3,)),
                 dma((pairs + 1,)), dma((pairs + 1,)), dma((pairs + 1,)), dma((pairs + 1,)), dma((2,)), dma((2,)),
                 dma((9,)), dma((9,)), dma((2, pairs)), dma((2, pairs)), dma((pairs,)), dma((pairs,)),
                 dma((pairs // 2,)), dma((pairs // 2,)),
             ],
             compiler_params=pltpu.CompilerParams(collective_id=0, has_side_effects=True, vmem_limit_bytes=55_000_000),
-        )(q_blk, kv_blk, len_blk)
+        )(*(pltpu.with_memory_space_constraint(x, pltpu.HBM) for x in (q_blk, kv_blk, len_blk)))
 
     return jax.shard_map(local_step, mesh=mesh, in_specs=(P('dp', None, 'dcp', None), P('dp', None, 'dcp', None, None), P('dp')),
                          out_specs=P('dp', None, 'dcp', None), check_vma=False)

time: 57.6 us -> 56.2 us (0.976)
  Pallas kernels: 55.8 us -> 55.1 us
  local copies, waits for them, and re-layouts: 1.63 us -> 0.97 us
    pallas_call x1, Pallas kernels: 55.8 us -> 55.1 us  [local_step(): pl.pallas_call(functools.partial(kernel, batch), out_shape=jax.ShapeDtype...]
    unnamed x3 -> x1, local copies, waits for them, and re-layouts: 1.63 us -> 0.97 us
where the time goes in v4:
time: 56.2 us; the launch traced here: 56.1 us
  Pallas kernels  55.1 us (98%)
  local copies, waits for them, and re-layouts  0.97 us (2%)
    pallas_call x1, Pallas kernels, local_step(): pl.pallas_call(functools.partial(kernel, batch), out_shape=jax.ShapeDtype...  55.1 us

profile of v4, /device:TPU:0, one launch (start us, length us, event | category | flops | bytes accessed | tf_op | source)
XLA Modules:
  0.0 56.1 jit_solution(15938531151244343294)
XLA Ops:
  0.0 55.1 %shard_map.37 = bf16[32,2,16,512]{3,2,1,0:T(8,128)(2,1)S(1)} custom-call(bf16[32,2,16,576]{3,2,1,0:T(8,128)(2,1)} %q_hbm.1, bf16[32,32,1,64,576]{4,3,2,1,0:T(8,128)(2,1)} %kv_hbm.1, s32[32]{0:T(128)} %len_hbm.1), custom_call_target="tpu_custom_call" | custom-call | tf_op jit(solution)/shard_map/pallas_call | solution.py:360
  55.1 1.0 %copy.5 = bf16[32,2,16,512]{3,2,1,0:T(8,128)(2,1)} copy(bf16[32,2,16,512]{3,2,1,0:T(8,128)(2,1)S(1)} %shard_map.37) | data formatting | bytes 2097152

commit v5 on v4

--- a/solution.py
+++ b/solution.py
@@ -262,13 +262,13 @@
             for d in o_peer(i - 1):
                 d.start()
         if not static or i >= 3:
-            o_cross(i - 3).start()
             if static and i % 2 == 0:
                 lse_cross((i - 4) // 2).start()
             if not static:
                 @pl.when(lax.rem(i, 2) == 0)
                 def _():
                     lse_cross((i - 4) // 2).start()
+            o_cross(i - 3).start()
         if not static or i + 2 <= pairs:
             single = static and i + 2 == pairs
             q_cross(i + 2, single).wait_recv()
@@ -293,15 +293,16 @@
     i = pairs - 1
     for d in o_peer(i):
         d.start()
+    lse_cross((i - 3) // 2).start()
     o_cross(i - 2).start()
-    lse_cross((i - 3) // 2).start()
     for j in (i - 1, i):
         for d in o_peer(j):
             d.wait_recv()
         for par in range(2):
             combine(j, par)
+        if j == i:
+            lse_cross((i - 1) // 2).start()
         o_cross(j).start()
-    lse_cross((i - 1) // 2).start()
 
     def drain_q(k, c):
         q_cross(k).wait_send()
@@ -327,9 +328,9 @@
 
     def final(g, c):
         lse_cross(g).wait_recv()
+        cols = []
         for u in range(2):
             i = 2 * g + u
-            o_cross(i).wait_recv()
             l1 = jnp.concatenate([fl[i, 0:1, :32], fl[i, 1:2, :32]], 1)
             l2 = cq[2 * g + 1][:, 64 * u:64 * u + 64]
             top = jnp.maximum(l1, l2)
@@ -337,11 +338,16 @@
             den = e1 + e2
             col = jnp.broadcast_to(jnp.concatenate([e1 / den, e2 / den], 1), (128, 128)).T
             for par in range(2):
-                c1 = jnp.concatenate([col[32 * par:32 * par + 32]] * 4, 1)
-                c2 = jnp.concatenate([col[64 + 32 * par:96 + 32 * par]] * 4, 1)
-                o = (c1 * fc[i, par] + c2 * cr[i, par].astype(F32)).astype(BF)
-                o_ref[2 * i + par] = o.reshape(2, 16, LATENT)
-            o_cross(i).wait_send()
+                fc[i, par] = fc[i, par] * jnp.concatenate([col[32 * par:32 * par + 32]] * 4, 1)
+            cols.append(col[64:])
+        for u in range(2):
+            i = 2 * g + u
+            o_cross(i).wait_recv()
+            for par in range(2):
+                c2 = jnp.concatenate([cols[u][32 * par:32 * par + 32]] * 4, 1)
+                o_ref[2 * i + par] = (fc[i, par] + c2 * cr[i, par].astype(F32)).astype(BF).reshape(2, 16, LATENT)
+        for u in range(2):
+            o_cross(2 * g + u).wait_send()
         lse_cross(g).wait_send()
         return c
 

time: 56.2 us -> 55.6 us (0.989)
  Pallas kernels: 55.1 us -> 54.5 us
    pallas_call x1, Pallas kernels: 55.1 us -> 54.5 us  [local_step(): pl.pallas_call(functools.partial(kernel, batch), out_shape=jax.ShapeDtype...]
where the time goes in v5:
time: 55.6 us; the launch traced here: 55.4 us
  Pallas kernels  54.5 us (98%)
  local copies, waits for them, and re-layouts  0.97 us (2%)
    pallas_call x1, Pallas kernels, local_step(): pl.pallas_call(functools.partial(kernel, batch), out_shape=jax.ShapeDtype...  54.5 us

profile of v5, /device:TPU:0, one launch (start us, length us, event | category | flops | bytes accessed | tf_op | source)
XLA Modules:
  0.0 55.4 jit_solution(2783657576073934144)
XLA Ops:
  0.0 54.5 %shard_map.37 = bf16[32,2,16,512]{3,2,1,0:T(8,128)(2,1)S(1)} custom-call(bf16[32,2,16,576]{3,2,1,0:T(8,128)(2,1)} %q_hbm.1, bf16[32,32,1,64,576]{4,3,2,1,0:T(8,128)(2,1)} %kv_hbm.1, s32[32]{0:T(128)} %len_hbm.1), custom_call_target="tpu_custom_call" | custom-call | tf_op jit(solution)/shard_map/pallas_call | solution.py:366
  54.5 1.0 %copy.5 = bf16[32,2,16,512]{3,2,1,0:T(8,128)(2,1)} copy(bf16[32,2,16,512]{3,2,1,0:T(8,128)(2,1)S(1)} %shard_map.37) | data formatting | bytes 2097152

commit v6 on v5

--- a/solution.py
+++ b/solution.py
@@ -83,11 +83,19 @@
         return (remote(so.at[i], to.at[i], o_ss.at[0, i], o_rs.at[0, i], peer),
                 remote(sl.at[i], tl.at[i], o_ss.at[1, i], o_rs.at[1, i], peer))
 
-    def o_cross(i):
-        return remote(co.at[i], cr.at[i], c_ss.at[i], c_rs.at[i], cross)
-
-    def lse_cross(g):
-        return remote(cl.at[2 * g + 1], cq.at[2 * g + 1], l_ss.at[g], l_rs.at[g], cross)
+    whole = pairs // 2 - 2
+
+    def o_cross(k):
+        r = pl.ds(whole + k, 1) if isinstance(k, int) and k >= whole else pl.ds(2 * k, 2)
+        return remote(co.at[r], cr.at[r], c_ss.at[k], c_rs.at[k], cross)
+
+    def lse_cross(k):
+        r = pl.ds(whole // 2 + k, 1) if isinstance(k, int) and k >= whole // 2 else pl.ds(2 * k, 2)
+        return remote(cl.at[r], cq.at[r], l_ss.at[k], l_rs.at[k], cross)
+
+    barrier = pltpu.get_barrier_semaphore()
+    for other in (cross, peer):
+        pl.semaphore_signal(barrier, inc=1, device_id=(dp, other), device_id_type=MESH)
 
     stage_first = pltpu.make_async_copy(q_hbm.at[pl.ds(0, 1)], stage.at[pl.ds(0, 1)], st_sem.at[0])
     stage_rest = pltpu.make_async_copy(q_hbm.at[pl.ds(1, batch - 1)], stage.at[pl.ds(1, batch - 1)], st_sem.at[1])
@@ -101,9 +109,6 @@
         ro[b] = jnp.concatenate([both[0], both[1]], axis=1)
         return c
 
-    barrier = pltpu.get_barrier_semaphore()
-    for other in (peer, cross):
-        pl.semaphore_signal(barrier, inc=1, device_id=(dp, other), device_id_type=MESH)
     pl.semaphore_wait(barrier, 2)
 
     for d in (q_cross(0, True), q_peer(0)):
@@ -215,7 +220,7 @@
         fl[i, par:par + 1, :] = lse
         if par == 1:
             before = lax.rem(i + dummy - 1, dummy)
-            cl[i] = jnp.concatenate([r[:, 32:64] for r in (fl[before, 0:1, :], fl[before, 1:2, :], fl[i, 0:1, :], lse)], 1)
+            cl[i // 2] = jnp.concatenate([r[:, 32:64] for r in (fl[before, 0:1, :], fl[before, 1:2, :], fl[i, 0:1, :], lse)], 1)
 
     for d in (q_cross(0, True), rope_cross(0)):
         d.wait_recv()
@@ -261,14 +266,20 @@
         if not static or i >= 1:
             for d in o_peer(i - 1):
                 d.start()
-        if not static or i >= 3:
-            if static and i % 2 == 0:
-                lse_cross((i - 4) // 2).start()
-            if not static:
-                @pl.when(lax.rem(i, 2) == 0)
-                def _():
-                    lse_cross((i - 4) // 2).start()
-            o_cross(i - 3).start()
+        if static and i + 1 == pairs:
+            o_cross(whole).start()
+        if not static:
+            @pl.when(lax.rem(i, 4) == 2)
+            def _():
+                lse_cross((i - 6) // 4).start()
+
+            @pl.when(lax.rem(i, 2) == 0)
+            def _():
+                o_cross((i - 4) // 2).start()
+        elif i >= 4 and i % 2 == 0:
+            if i % 4 == 2:
+                lse_cross((i - 6) // 4).start()
+            o_cross((i - 4) // 2).start()
         if not static or i + 2 <= pairs:
             single = static and i + 2 == pairs
             q_cross(i + 2, single).wait_recv()
@@ -293,16 +304,16 @@
     i = pairs - 1
     for d in o_peer(i):
         d.start()
-    lse_cross((i - 3) // 2).start()
-    o_cross(i - 2).start()
+    lse_cross(whole // 2).start()
+    o_cross(whole + 1).start()
     for j in (i - 1, i):
         for d in o_peer(j):
             d.wait_recv()
         for par in range(2):
             combine(j, par)
         if j == i:
-            lse_cross((i - 1) // 2).start()
-        o_cross(j).start()
+            lse_cross(whole // 2 + 1).start()
+        o_cross(j - whole).start()
 
     def drain_q(k, c):
         q_cross(k).wait_send()
@@ -326,13 +337,12 @@
 
     lax.fori_loop(0, pairs, drain_peer, 0)
 
-    def final(g, c):
-        lse_cross(g).wait_recv()
+    def final(g, parts):
         cols = []
         for u in range(2):
             i = 2 * g + u
             l1 = jnp.concatenate([fl[i, 0:1, :32], fl[i, 1:2, :32]], 1)
-            l2 = cq[2 * g + 1][:, 64 * u:64 * u + 64]
+            l2 = cq[g][:, 64 * u:64 * u + 64]
             top = jnp.maximum(l1, l2)
             e1, e2 = jnp.exp2(l1 - top), jnp.exp2(l2 - top)
             den = e1 + e2
@@ -342,16 +352,28 @@
             cols.append(col[64:])
         for u in range(2):
             i = 2 * g + u
-            o_cross(i).wait_recv()
+            if u < len(parts):
+                parts[u].wait_recv()
             for par in range(2):
                 c2 = jnp.concatenate([cols[u][32 * par:32 * par + 32]] * 4, 1)
                 o_ref[2 * i + par] = (fc[i, par] + c2 * cr[i, par].astype(F32)).astype(BF).reshape(2, 16, LATENT)
-        for u in range(2):
-            o_cross(2 * g + u).wait_send()
-        lse_cross(g).wait_send()
-        return c
-
-    lax.fori_loop(0, pairs // 2, final, 0)
+
+    def final_loop(k, c):
+        lse_cross(k).wait()
+        for h in range(2):
+            final(2 * k + h, (o_cross(2 * k + h),))
+        for h in range(2):
+            o_cross(2 * k + h).wait_send()
+        return c
+
+    lax.fori_loop(0, whole // 2, final_loop, 0)
+    for h in range(2):
+        lse_cross(whole // 2 + h).wait_recv()
+        final(whole + h, (o_cross(whole + 2 * h), o_cross(whole + 2 * h + 1)))
+    for h in range(2):
+        lse_cross(whole // 2 + h).wait_send()
+    for h in range(4):
+        o_cross(whole + h).wait_send()
 
 
 def solution(mesh):
@@ -378,12 +400,11 @@
                 vm((16, 128, 128), BF), vm((16, 128, 128), BF),
                 vm((n, 2, 64, LATENT), BF), vm((n, 2, 64, LATENT), BF), vm((n, 2, 64, LATENT), BF),
                 vm((n, 2, 128), F32), vm((n, 2, 128), F32), vm((n, 2, 128), F32),
-                vm((n, 2, 32, LATENT), BF), vm((n, 1, 128), F32), vm((n, 2, 32, LATENT), BF), vm((n, 1, 128), F32),
+                vm((n, 2, 32, LATENT), BF), vm((n // 2, 1, 128), F32), vm((n, 2, 32, LATENT), BF), vm((n // 2, 1, 128), F32),
                 vm((n, 2, 32, LATENT), F32), vm((n, 2, 128), F32),
                 dma((KV_SLOTS // 2,)), dma((3,)),
                 dma((pairs + 1,)), dma((pairs + 1,)), dma((pairs + 1,)), dma((pairs + 1,)), dma((2,)), dma((2,)),
-                dma((9,)), dma((9,)), dma((2, pairs)), dma((2, pairs)), dma((pairs,)), dma((pairs,)),
-                dma((pairs // 2,)), dma((pairs // 2,)),
+                dma((9,)), dma((9,)), dma((2, pairs)), dma((2, pairs)), dma((10,)), dma((10,)), dma((5,)), dma((5,)),
             ],
             compiler_params=pltpu.CompilerParams(collective_id=0, has_side_effects=True, vmem_limit_bytes=55_000_000),
         )(*(pltpu.with_memory_space_constraint(x, pltpu.HBM) for x in (q_blk, kv_blk, len_blk)))

time: 55.6 us -> 55.3 us (level)
  no operation moved by 1% of the time
where the time goes in v6:
time: 55.3 us; the launch traced here: 55.2 us
  Pallas kernels  54.2 us (98%)
  local copies, waits for them, and re-layouts  0.97 us (2%)
    pallas_call x1, Pallas kernels, local_step(): pl.pallas_call(functools.partial(kernel, batch), out_shape=jax.ShapeDtype...  54.2 us

profile of v6, /device:TPU:0, one launch (start us, length us, event | category | flops | bytes accessed | tf_op | source)
XLA Modules:
  0.0 55.2 jit_solution(5692733726842846401)
XLA Ops:
  0.0 54.2 %shard_map.37 = bf16[32,2,16,512]{3,2,1,0:T(8,128)(2,1)S(1)} custom-call(bf16[32,2,16,576]{3,2,1,0:T(8,128)(2,1)} %q_hbm.1, bf16[32,32,1,64,576]{4,3,2,1,0:T(8,128)(2,1)} %kv_hbm.1, s32[32]{0:T(128)} %len_hbm.1), custom_call_target="tpu_custom_call" | custom-call | tf_op jit(solution)/shard_map/pallas_call | solution.py:388
  54.2 1.0 %copy.5 = bf16[32,2,16,512]{3,2,1,0:T(8,128)(2,1)} copy(bf16[32,2,16,512]{3,2,1,0:T(8,128)(2,1)S(1)} %shard_map.37) | data formatting | bytes 2097152
